TPU v7x, 128 devices: a whole 4x4x4 slice. The times are simulated.
128 devices in a mesh: mx: 4 (over z), my: 4 (over y_hi, core), col: 8 (over y_lo, x).
Axes of the slice: x: 4, y: 4 (y_hi: 2, y_lo: 2; y = y_hi * 2 + y_lo), z: 4, core: 2. Of those that a mesh axis runs over, the one named last changes fastest.
Arguments:
- spectrum: float32 [2, 16, 128, 32, 512], P(None, 'col', None, 'mx', 'my'), may hold values from -6 to 6
- core_tensor: float32 [2, 64, 64, 16, 16, 16], P(None, 'col', None, ('mx', 'my')), may hold values from -0.01171875 to 0.01171875
- input_factor: float32 [128, 64], replicated, may hold values from -0.5 to 0.5
- output_factor: float32 [128, 64], replicated, may hold values from -0.75 to 0.75
- first_factor: float32 [32, 16], P('mx'), may hold values from -5 to 5
- second_factor: float32 [32, 16], P('my'), may hold values from -5 to 5
- third_factor: float32 [16, 16], replicated, may hold values from -5 to 5
Outputs:
- mixed_modes: float32 [2, 16, 128, 32, 512], P(None, 'col', None, 'mx', 'my')
All inputs are finite; a program needn't handle non-finite values.
Results may differ from a plain program's by a relative error of at most 0.00007.
Values sent between devices are 32-bit elements; how exact they have to be, the bound alone decides.
No kernel may reach another device: no remote copies, remote signals or barrier semaphores. Data moves between devices by JAX's collectives and lax.ppermute only.
A program may use at most 128 MiB of HBM per device.

v0:
```python
import jax
import jax.numpy as jnp
from jax import lax
from jax.sharding import PartitionSpec as P

precise = lax.Precision.HIGHEST


def per_device(
    spectrum, core_tensor, input_factor, output_factor, first_factor, second_factor, third_factor
):
    rank_local = core_tensor.shape[1]
    rank_out = core_tensor.shape[2]
    rows_first = first_factor.shape[0]
    rank_second = second_factor.shape[1]
    modes_third = third_factor.shape[0]
    core_third = jnp.einsum("cpqstu,zu->cpqstz", core_tensor, third_factor, precision=precise)
    core_third = core_third.reshape(
        2, rank_local, rank_out, core_tensor.shape[3], rank_second * modes_third
    )
    core_gathered = lax.all_gather(core_third, ("mx", "my"), axis=3, tiled=True)
    weight_first = jnp.einsum("cpqsm,ks->cpqkm", core_gathered, first_factor, precision=precise)
    weight_first = weight_first.reshape(
        2, rank_local, rank_out, rows_first, rank_second, modes_third
    )
    mode_weight = jnp.einsum("cpqktz,yt->cpqkyz", weight_first, second_factor, precision=precise)
    mode_weight = mode_weight.reshape(2, rank_local, rank_out, rows_first, -1)
    projected = jnp.einsum("cbikm,ir->cbrkm", spectrum, input_factor, precision=precise)
    rank_spectrum = lax.all_to_all(projected, "col", split_axis=2, concat_axis=1, tiled=True)
    real_part = jnp.einsum(
        "brkm,rqkm->bqkm", rank_spectrum[0], mode_weight[0], precision=precise
    ) - jnp.einsum("brkm,rqkm->bqkm", rank_spectrum[1], mode_weight[1], precision=precise)
    imag_part = jnp.einsum(
        "brkm,rqkm->bqkm", rank_spectrum[0], mode_weight[1], precision=precise
    ) + jnp.einsum("brkm,rqkm->bqkm", rank_spectrum[1], mode_weight[0], precision=precise)
    mode_values = jnp.stack([real_part, imag_part])
    summed_values = lax.psum_scatter(mode_values, "col", scatter_dimension=1, tiled=True)
    mixed_modes = jnp.einsum("oq,cbqkm->cbokm", output_factor, summed_values, precision=precise)
    return mixed_modes


def solution(mesh):
    placed = (
        P(None, "col", None, "mx", "my"),
        P(None, "col", None, ("mx", "my"), None, None),
        P(),
        P(),
        P("mx", None),
        P("my", None),
        P(),
    )
    return jax.shard_map(
        per_device,
        mesh=mesh,
        in_specs=placed,
        out_specs=P(None, "col", None, "mx", "my"),
        check_vma=False,
    )
```

profile of v0, /device:TPU:1, one launch (start us, length us, event | category | flops | bytes accessed | tf_op | source)
XLA Modules:
  0.0 377.2 jit_solution(9555578541024835973)
XLA Ops:
  6.5 1.6 copy-done
  8.1 3.9 %fusion.22 = f32[2,8,64,16,16]{2,4,3,1,0:T(8,128)} fusion(f32[2,8,64,1,16,16]{2,5,4,3,1,0:T(8,128)S(1)} %copy-done, f32[16,16]{1,0:T(8,128)} %param.13), kind=kOutput, calls=%fused_computation.17 | convolution fusion | flops 50331648 | bytes 2098176 | tf_op jit(solution)/shard_map/cpqstu,zu->cpqstz/dot_general | solution.py:17
  12.1 3.2 copy.51
  15.2 0.0 all-gather.2.cloned.1.call-update
  15.2 0.0 reduce-scatter.2.cloned.1.call-start
  15.3 3.1 fusion.26
  18.4 0.6 copy.57
  19.0 20.6 %all_to_all.15 = f32[2,2,64,8,128]{4,3,1,0,2:T(8,128)S(1)} all-to-all(f32[2,2,64,8,128]{4,3,1,0,2:T(8,128)S(1)} %copy.57), channel_id=1, replica_groups=mesh['mx'=4,'my'=4,'col'=8] {'col'}, dimensions={2} | all-to-all | bytes 2097152 | tf_op jit(solution)/shard_map/all_to_all | solution.py:29
  39.6 0.1 copy.58
  39.7 0.1 fusion.36
  39.9 0.0 copy-start.6
  39.9 3.2 copy.61
  43.1 3.1 copy.65
  46.2 90.1 %all-gather.2.cloned.1.call-done = f32[2,8,64,16,256]{4,2,1,0,3:T(8,128)} async-done(((f32[2,8,64,1,256]{4,2,1,0,3:T(8,128)}), f32[2,8,64,16,256]{4,2,1,0,3:T(8,128)}) %all-gather.2.cloned.1.call-update) | async-done | bytes 16777232 | tf_op jit(solution)/shard_map/all_gather | solution.py:21
  136.3 25.8 %fusion.16 = f32[2,8,64,8,256]{4,3,2,1,0:T(8,128)} fusion(f32[2,8,64,16,256]{4,2,1,0,3:T(8,128)} %all-gather.2.cloned.1.call-done, f32[8,16]{1,0:T(8,128)S(1)} %copy-done.6), kind=kOutput, calls=%fused_computation.15 | convolution fusion | flops 402653184 | bytes 25166336 | tf_op jit(solution)/shard_map/cpqsm,ks->cpqkm/dot_general | solution.py:22
  162.1 12.2 %copy.53 = f32[2,8,64,8,256]{2,4,3,1,0:T(8,128)} copy(f32[2,8,64,8,256]{4,3,2,1,0:T(8,128)} %fusion.16) | data formatting | bytes 16777216 | tf_op jit(solution)/shard_map/cpqsm,ks->cpqkm/transpose | solution.py:22
  174.4 17.9 %fusion.19 = f32[2,8,64,8,8,16]{2,4,5,3,1,0:T(8,128)S(1)} fusion(f32[2,8,64,8,16,16]{2,5,4,3,1,0:T(8,128)} %bitcast.59, f32[8,16]{1,0:T(8,128)S(1)} %copy-done.7), kind=kOutput, calls=%fused_computation.16 | convolution fusion | flops 201326592 | bytes 12583424 | tf_op jit(solution)/shard_map/cpqktz,yt->cpqkyz/dot_general | solution.py:26
  192.2 1.1 fusion.35
  193.3 0.9 copy.55
  194.2 0.9 copy.62
  195.2 1.2 copy-done.2
  196.4 14.4 %fusion.4 = f32[8,128,64,16]{2,3,1,0:T(8,128)S(1)} fusion(f32[16,8,8,128]{0,1,3,2:T(8,128)S(1)} %copy-done.2, f32[8,64,8,128]{1,3,2,0:T(8,128)S(1)} %bitcast.60), kind=kOutput, calls=%fused_computation.7 | convolution fusion | flops 100663296 | bytes 6815744 | tf_op jit(solution)/shard_map/brkm,rqkm->bqkm/dot_general | solution.py:33
  210.8 14.6 %fusion.6 = f32[8,128,64,16]{2,3,1,0:T(8,128)S(1)} fusion(f32[16,8,8,128]{0,1,3,2:T(8,128)S(1)} %copy-done.3, f32[8,64,8,128]{1,3,2,0:T(8,128)S(1)} %bitcast.61), kind=kOutput, calls=%fused_computation.9 | convolution fusion | flops 100663296 | bytes 6815744 | tf_op jit(solution)/shard_map/brkm,rqkm->bqkm/dot_general | solution.py:32
  225.4 14.3 %add_bitcast_fusion = f32[1,16,64,8,128]{2,1,4,3,0:T(8,128)S(1)} fusion(f32[8,128,64,16]{2,3,1,0:T(8,128)S(1)} %fusion.4, f32[16,8,8,128]{0,1,3,2:T(8,128)S(1)} %copy-done.3, f32[8,64,8,128]{1,3,2,0:T(8,128)S(1)} %bitcast.57), kind=kOutput, calls=%fused_computation.5 | convolution fusion | flops 101711872 | bytes 11010048 | tf_op jit(solution)/shard_map/brkm,rqkm->bqkm/dot_general | solution.py:35
  239.8 14.4 %subtract_bitcast_fusion = f32[1,16,64,8,128]{2,1,4,3,0:T(8,128)S(1)} fusion(f32[8,128,64,16]{2,3,1,0:T(8,128)S(1)} %fusion.6, f32[16,8,8,128]{0,1,3,2:T(8,128)S(1)} %copy-done.2, f32[8,64,8,128]{1,3,2,0:T(8,128)S(1)} %bitcast.58), kind=kOutput, calls=%fused_computation.6 | convolution fusion | flops 101711872 | bytes 11010048 | tf_op jit(solution)/shard_map/brkm,rqkm->bqkm/dot_general | solution.py:30
  254.2 6.1 %pad_maximum_fusion = f32[2,16,64,8,128]{2,1,4,3,0:T(8,128)} fusion(f32[1,16,64,8,128]{2,1,4,3,0:T(8,128)S(1)} %add_bitcast_fusion, f32[1,16,64,8,128]{2,1,4,3,0:T(8,128)S(1)} %subtract_bitcast_fusion), kind=kLoop, calls=%fused_computation | loop fusion | flops 2097152 | bytes 16777216 | tf_op jit(solution)/shard_map/stack | solution.py:36
  260.3 11.0 %copy.70 = f32[2,16,64,8,128]{4,3,2,0,1:T(8,128)} copy(f32[2,16,64,8,128]{2,1,4,3,0:T(8,128)} %pad_maximum_fusion) | data formatting | bytes 16777216 | tf_op jit(solution)/shard_map/stack | solution.py:36
  271.3 0.0 copy-start.5
  271.3 0.0 reduce-scatter.2.cloned.1.call-update
  271.3 89.9 %reduce-scatter.2.cloned.1.call-done = f32[2,2,64,8,128]{4,3,2,0,1:T(8,128)} async-done(((f32[2,16,64,8,128]{4,3,2,0,1:T(8,128)}), f32[2,2,64,8,128]{4,3,2,0,1:T(8,128)}) %reduce-scatter.2.cloned.1.call-update) | async-done | bytes 1048592 | tf_op jit(solution)/shard_map/reduce_scatter | solution.py:37
  361.2 6.0 %convolution_bitcast_fusion = f32[2,2,128,8,128]{2,4,3,1,0:T(8,128)} fusion(f32[2,2,64,8,128]{4,3,2,0,1:T(8,128)} %reduce-scatter.2.cloned.1.call-done, f32[128,64]{0,1:T(8,128)S(1)} %copy-done.5), kind=kOutput, calls=%fused_computation.21 | convolution fusion | flops 402653184 | bytes 3178496 | tf_op jit(solution)/shard_map/oq,cbqkm->cbokm/dot_general | solution.py:38
  367.2 2.9 copy.72
  (15 shorter events, 0.1 us)
Async XLA Ops:
  6.5 1.6 copy-start
  6.5 8.8 %copy-start.4 = (f32[128,64]{0,1:T(8,128)S(1)}, f32[128,64]{0,1:T(8,128)}, u32[]{:S(2)}) copy-start(f32[128,64]{0,1:T(8,128)} %param.9) | copy-start | bytes 98308
  6.5 129.7 %all-gather.2.cloned.1.call-start = ((), (), s32[]{:S(2)}) async-start(), calls=%async_computation.2 | async-start | bytes 17825792 | tf_op jit(solution)/shard_map/all_gather | solution.py:21
  15.2 346.0 %reduce-scatter.2.cloned.1.call-start = ((), (), s32[]{:S(2)}) async-start(), calls=%async_computation.3 | async-start | bytes 9437184 | tf_op jit(solution)/shard_map/reduce_scatter | solution.py:37
  39.9 96.3 %copy-start.6 = (f32[8,16]{1,0:T(8,128)S(1)}, f32[8,16]{1,0:T(8,128)}, u32[]{:S(2)}) copy-start(f32[8,16]{1,0:T(8,128)} %param.11) | copy-start | bytes 1540
  162.1 12.2 %copy-start.7 = (f32[8,16]{1,0:T(8,128)S(1)}, f32[8,16]{1,0:T(8,128)}, u32[]{:S(2)}) copy-start(f32[8,16]{1,0:T(8,128)} %param.12) | copy-start | bytes 1540
  194.2 2.2 copy-start.2
  196.4 14.4 %copy-start.3 = (f32[16,8,8,128]{0,1,3,2:T(8,128)S(1)}, f32[16,8,8,128]{0,1,3,2:T(8,128)}, u32[]{:S(2)}) copy-start(f32[16,8,8,128]{0,1,3,2:T(8,128)} %copy.65) | copy-start | bytes 1572868
  271.3 89.9 %copy-start.5 = (f32[128,64]{0,1:T(8,128)S(1)}, f32[128,64]{0,1:T(8,128)}, u32[]{:S(2)}) copy-start(f32[128,64]{0,1:T(8,128)} %param.10) | copy-start | bytes 98308
  271.3 98.8 %copy-start.1 = (f32[2,8,64,1,16,16]{2,5,4,3,1,0:T(8,128)S(1)}, f32[2,8,64,1,16,16]{2,5,4,3,1,0:T(8,128)}, u32[]{:S(2)}) copy-start(f32[2,8,64,1,16,16]{2,5,4,3,1,0:T(8,128)} %param.8) | copy-start | bytes 3145732
Sparse Core Ops, SparseCore 0:
  15.4 120.8 all-gather.1
  271.4 89.7 reduce-scatter.1
where the time goes:
time: 383 us; the launch traced here: 377 us
  waiting for transfers between devices  180 us (47%)
  matrix products  114 us (30%)
  local copies, waits for them, and re-layouts  42.2 us (11%)
  blocking collectives  20.6 us (5%)
  between operations  13.8 us (4%)
  other arithmetic  6.1 us (2%)
    all_gather x1, waiting for transfers between devices, per_device(): core_gathered = lax.all_gather(core_third, ('mx', 'my'), axis=3, tiled=True)  90.1 us
    reduce_scatter x1, waiting for transfers between devices, per_device(): lax.psum_scatter(mode_values, 'col', scatter_dimension=1, tiled=True)  89.9 us
    dot_general x1, matrix products, per_device(): jnp.einsum('cpqsm,ks->cpqkm', core_gathered, first_factor, precision=prec...  25.8 us
    all_to_all x1, blocking collectives, per_device(): lax.all_to_all(projected, 'col', split_axis=2, concat_axis=1, tiled=True)  20.6 us
    dot_general x1, matrix products, per_device(): jnp.einsum('cpqktz,yt->cpqkyz', weight_first, second_factor, precision=pr...  17.9 us
    dot_general x1, matrix products, per_device(): jnp.einsum('brkm,rqkm->bqkm', rank_spectrum[1], mode_weight[1], precision...  14.6 us
    dot_general x1, matrix products, per_device(): jnp.einsum('brkm,rqkm->bqkm', rank_spectrum[0], mode_weight[1], precision...  14.4 us
    dot_general x1, matrix products, per_device(): jnp.einsum('brkm,rqkm->bqkm', rank_spectrum[0], mode_weight[0], precision...  14.4 us
  transfers between devices with their start and end apart: 2, of which 2 were waited for; matrix products, arithmetic and copies ran while one was open for 3% of the time, Pallas kernels for 0%

commit v1 on v0

--- a/solution.py
+++ b/solution.py
@@ -26,7 +26,10 @@
     mode_weight = jnp.einsum("cpqktz,yt->cpqkyz", weight_first, second_factor, precision=precise)
     mode_weight = mode_weight.reshape(2, rank_local, rank_out, rows_first, -1)
     projected = jnp.einsum("cbikm,ir->cbrkm", spectrum, input_factor, precision=precise)
-    rank_spectrum = lax.all_to_all(projected, "col", split_axis=2, concat_axis=1, tiled=True)
+    rank_spectrum = jnp.concatenate(
+        lax.all_to_all(jnp.stack(jnp.split(projected, lax.axis_size("col"), axis=2)), "col", 0, 0),
+        axis=1,
+    )
     real_part = jnp.einsum(
         "brkm,rqkm->bqkm", rank_spectrum[0], mode_weight[0], precision=precise
     ) - jnp.einsum("brkm,rqkm->bqkm", rank_spectrum[1], mode_weight[1], precision=precise)

time: 383 us -> 381 us (level)
  transfers between devices with their start and end apart: 2 -> 2, of which waited for: 2 -> 2; matrix products, arithmetic and copies ran while one was open for 3% -> 2% of each run, Pallas kernels for 0% -> 0%
where the time goes in v1:
time: 381 us; the launch traced here: 377 us
  waiting for transfers between devices  181 us (48%)
  matrix products  114 us (30%)
  local copies, waits for them, and re-layouts  40.7 us (11%)
  blocking collectives  20.8 us (5%)
  between operations  13.9 us (4%)
  other arithmetic  6.1 us (2%)
    all_gather x1, waiting for transfers between devices, per_device(): core_gathered = lax.all_gather(core_third, ('mx', 'my'), axis=3, tiled=True)  91.2 us
    reduce_scatter x1, waiting for transfers between devices, per_device(): lax.psum_scatter(mode_values, 'col', scatter_dimension=1, tiled=True)  89.9 us
    dot_general x1, matrix products, per_device(): jnp.einsum('cpqsm,ks->cpqkm', core_gathered, first_factor, precision=prec...  25.7 us
    all_to_all x1, blocking collectives, per_device(): lax.all_to_all(jnp.stack(jnp.split(projected, lax.axis_size('col'), axis=...  20.8 us
    dot_general x1, matrix products, per_device(): jnp.einsum('cpqktz,yt->cpqkyz', weight_first, second_factor, precision=pr...  17.7 us
    dot_general x1, matrix products, per_device(): jnp.einsum('brkm,rqkm->bqkm', rank_spectrum[1], mode_weight[1], precision...  14.6 us
    dot_general x1, matrix products, per_device(): jnp.einsum('brkm,rqkm->bqkm', rank_spectrum[0], mode_weight[1], precision...  14.4 us
    dot_general x1, matrix products, per_device(): jnp.einsum('brkm,rqkm->bqkm', rank_spectrum[0], mode_weight[0], precision...  14.4 us
  transfers between devices with their start and end apart: 2, of which 2 were waited for; matrix products, arithmetic and copies ran while one was open for 2% of the time, Pallas kernels for 0%

profile of v1, /device:TPU:1, one launch (start us, length us, event | category | flops | bytes accessed | tf_op | source)
XLA Modules:
  0.0 376.8 jit_solution(9017947949962841470)
XLA Ops:
  6.5 0.0 copy-start
  6.5 1.6 copy-done
  8.1 3.9 %fusion.22 = f32[2,8,64,16,16]{2,4,3,1,0:T(8,128)} fusion(f32[2,8,64,1,16,16]{2,5,4,3,1,0:T(8,128)S(1)} %copy-done, f32[16,16]{1,0:T(8,128)} %param.13), kind=kOutput, calls=%fused_computation.17 | convolution fusion | flops 50331648 | bytes 2098176 | tf_op jit(solution)/shard_map/cpqstu,zu->cpqstz/dot_general | solution.py:17
  12.1 3.2 copy.33
  15.2 0.0 all-gather.2.cloned.1.call-update
  15.2 0.0 reduce-scatter.2.cloned.1.call-start
  15.3 3.1 fusion.26
  18.6 20.8 %all_to_all.5 = f32[8,2,2,8,8,128]{5,3,4,2,1,0:T(8,128)S(1)} all-to-all(f32[8,2,2,8,8,128]{5,3,4,2,1,0:T(8,128)S(1)} %fusion.30), channel_id=1, replica_groups=mesh['mx'=4,'my'=4,'col'=8] {'col'}, dimensions={0} | all-to-all | bytes 2097152 | tf_op jit(solution)/shard_map/all_to_all | solution.py:30
  39.4 0.1 fusion.44
  39.6 0.0 copy-start.6
  39.6 2.6 copy.40
  42.2 2.6 copy.43
  44.8 91.2 %all-gather.2.cloned.1.call-done = f32[2,8,64,16,256]{4,2,1,0,3:T(8,128)} async-done(((f32[2,8,64,1,256]{4,2,1,0,3:T(8,128)}), f32[2,8,64,16,256]{4,2,1,0,3:T(8,128)}) %all-gather.2.cloned.1.call-update) | async-done | bytes 16777232 | tf_op jit(solution)/shard_map/all_gather | solution.py:21
  136.1 25.7 %fusion.16 = f32[2,8,64,8,256]{4,3,2,1,0:T(8,128)} fusion(f32[2,8,64,16,256]{4,2,1,0,3:T(8,128)} %all-gather.2.cloned.1.call-done, f32[8,16]{1,0:T(8,128)S(1)} %copy-done.6), kind=kOutput, calls=%fused_computation.15 | convolution fusion | flops 402653184 | bytes 25166336 | tf_op jit(solution)/shard_map/cpqsm,ks->cpqkm/dot_general | solution.py:22
  161.8 12.4 %copy.35 = f32[2,8,64,8,256]{2,4,3,1,0:T(8,128)} copy(f32[2,8,64,8,256]{4,3,2,1,0:T(8,128)} %fusion.16) | data formatting | bytes 16777216 | tf_op jit(solution)/shard_map/cpqsm,ks->cpqkm/transpose | solution.py:22
  174.2 17.7 %fusion.19 = f32[2,8,64,8,8,16]{2,4,5,3,1,0:T(8,128)S(1)} fusion(f32[2,8,64,8,16,16]{2,5,4,3,1,0:T(8,128)} %bitcast.89, f32[8,16]{1,0:T(8,128)S(1)} %copy-done.7), kind=kOutput, calls=%fused_computation.16 | convolution fusion | flops 201326592 | bytes 12583424 | tf_op jit(solution)/shard_map/cpqktz,yt->cpqkyz/dot_general | solution.py:26
  191.9 1.1 fusion.43
  192.9 0.9 copy.37
  193.9 0.9 copy.41
  194.8 1.2 copy-done.2
  196.0 14.4 %fusion.4 = f32[8,128,64,16]{2,3,1,0:T(8,128)S(1)} fusion(f32[16,8,8,128]{0,1,3,2:T(8,128)S(1)} %copy-done.2, f32[8,64,8,128]{1,3,2,0:T(8,128)S(1)} %bitcast.90), kind=kOutput, calls=%fused_computation.7 | convolution fusion | flops 100663296 | bytes 6815744 | tf_op jit(solution)/shard_map/brkm,rqkm->bqkm/dot_general | solution.py:36
  210.4 14.6 %fusion.6 = f32[8,128,64,16]{2,3,1,0:T(8,128)S(1)} fusion(f32[16,8,8,128]{0,1,3,2:T(8,128)S(1)} %copy-done.3, f32[8,64,8,128]{1,3,2,0:T(8,128)S(1)} %bitcast.91), kind=kOutput, calls=%fused_computation.9 | convolution fusion | flops 100663296 | bytes 6815744 | tf_op jit(solution)/shard_map/brkm,rqkm->bqkm/dot_general | solution.py:35
  225.1 14.3 %add_bitcast_fusion = f32[1,16,64,8,128]{2,1,4,3,0:T(8,128)S(1)} fusion(f32[8,128,64,16]{2,3,1,0:T(8,128)S(1)} %fusion.4, f32[16,8,8,128]{0,1,3,2:T(8,128)S(1)} %copy-done.3, f32[8,64,8,128]{1,3,2,0:T(8,128)S(1)} %bitcast.87), kind=kOutput, calls=%fused_computation.5 | convolution fusion | flops 101711872 | bytes 11010048 | tf_op jit(solution)/shard_map/brkm,rqkm->bqkm/dot_general | solution.py:38
  239.4 14.4 %subtract_bitcast_fusion = f32[1,16,64,8,128]{2,1,4,3,0:T(8,128)S(1)} fusion(f32[8,128,64,16]{2,3,1,0:T(8,128)S(1)} %fusion.6, f32[16,8,8,128]{0,1,3,2:T(8,128)S(1)} %copy-done.2, f32[8,64,8,128]{1,3,2,0:T(8,128)S(1)} %bitcast.88), kind=kOutput, calls=%fused_computation.6 | convolution fusion | flops 101711872 | bytes 11010048 | tf_op jit(solution)/shard_map/brkm,rqkm->bqkm/dot_general | solution.py:33
  253.8 6.1 %pad_maximum_fusion = f32[2,16,64,8,128]{2,1,4,3,0:T(8,128)} fusion(f32[1,16,64,8,128]{2,1,4,3,0:T(8,128)S(1)} %add_bitcast_fusion, f32[1,16,64,8,128]{2,1,4,3,0:T(8,128)S(1)} %subtract_bitcast_fusion), kind=kLoop, calls=%fused_computation | loop fusion | flops 2097152 | bytes 16777216 | tf_op jit(solution)/shard_map/stack | solution.py:39
  259.9 11.0 %copy.48 = f32[2,16,64,8,128]{4,3,2,0,1:T(8,128)} copy(f32[2,16,64,8,128]{2,1,4,3,0:T(8,128)} %pad_maximum_fusion) | data formatting | bytes 16777216 | tf_op jit(solution)/shard_map/stack | solution.py:39
  270.9 0.0 copy-start.5
  270.9 0.0 reduce-scatter.2.cloned.1.call-update
  270.9 0.0 copy-start.1
  270.9 89.9 %reduce-scatter.2.cloned.1.call-done = f32[2,2,64,8,128]{4,3,2,0,1:T(8,128)} async-done(((f32[2,16,64,8,128]{4,3,2,0,1:T(8,128)}), f32[2,2,64,8,128]{4,3,2,0,1:T(8,128)}) %reduce-scatter.2.cloned.1.call-update) | async-done | bytes 1048592 | tf_op jit(solution)/shard_map/reduce_scatter | solution.py:40
  360.8 6.0 %convolution_bitcast_fusion = f32[2,2,128,8,128]{2,4,3,1,0:T(8,128)} fusion(f32[2,2,64,8,128]{4,3,2,0,1:T(8,128)} %reduce-scatter.2.cloned.1.call-done, f32[128,64]{0,1:T(8,128)S(1)} %copy-done.5), kind=kOutput, calls=%fused_computation.21 | convolution fusion | flops 402653184 | bytes 3178496 | tf_op jit(solution)/shard_map/oq,cbqkm->cbokm/dot_general | solution.py:41
  366.8 2.9 copy.50
  (19 shorter events, 0.2 us)
Async XLA Ops:
  6.5 1.6 copy-start
  6.5 8.8 %copy-start.4 = (f32[128,64]{0,1:T(8,128)S(1)}, f32[128,64]{0,1:T(8,128)}, u32[]{:S(2)}) copy-start(f32[128,64]{0,1:T(8,128)} %param.9) | copy-start | bytes 98308
  6.5 129.5 %all-gather.2.cloned.1.call-start = ((), (), s32[]{:S(2)}) async-start(), calls=%async_computation.2 | async-start | bytes 17825792 | tf_op jit(solution)/shard_map/all_gather | solution.py:21
  15.2 345.6 %reduce-scatter.2.cloned.1.call-start = ((), (), s32[]{:S(2)}) async-start(), calls=%async_computation.3 | async-start | bytes 9437184 | tf_op jit(solution)/shard_map/reduce_scatter | solution.py:40
  39.6 96.5 %copy-start.6 = (f32[8,16]{1,0:T(8,128)S(1)}, f32[8,16]{1,0:T(8,128)}, u32[]{:S(2)}) copy-start(f32[8,16]{1,0:T(8,128)} %param.11) | copy-start | bytes 1540
  161.8 12.4 %copy-start.7 = (f32[8,16]{1,0:T(8,128)S(1)}, f32[8,16]{1,0:T(8,128)}, u32[]{:S(2)}) copy-start(f32[8,16]{1,0:T(8,128)} %param.12) | copy-start | bytes 1540
  193.9 2.2 copy-start.2
  196.0 14.4 %copy-start.3 = (f32[16,8,8,128]{0,1,3,2:T(8,128)S(1)}, f32[16,8,8,128]{0,1,3,2:T(8,128)}, u32[]{:S(2)}) copy-start(f32[16,8,8,128]{0,1,3,2:T(8,128)} %copy.43) | copy-start | bytes 1572868
  270.9 89.9 %copy-start.5 = (f32[128,64]{0,1:T(8,128)S(1)}, f32[128,64]{0,1:T(8,128)}, u32[]{:S(2)}) copy-start(f32[128,64]{0,1:T(8,128)} %param.10) | copy-start | bytes 98308
  270.9 98.8 %copy-start.1 = (f32[2,8,64,1,16,16]{2,5,4,3,1,0:T(8,128)S(1)}, f32[2,8,64,1,16,16]{2,5,4,3,1,0:T(8,128)}, u32[]{:S(2)}) copy-start(f32[2,8,64,1,16,16]{2,5,4,3,1,0:T(8,128)} %param.8) | copy-start | bytes 3145732
Sparse Core Ops, SparseCore 0:
  15.4 120.6 all-gather.1
  271.0 89.7 reduce-scatter.1
